TPU v7x, 32 devices: a whole 2x2x4 slice. The times are simulated.
32 devices in a mesh: row: 4 (over y, x), col: 4 (over z), trial: 2 (over core).
Axes of the slice: x: 2, y: 2, z: 4, core: 2. Of those that a mesh axis runs over, the one named last changes fastest.
Arguments:
- pair_rows: bfloat16 [192, 96, 128], P(('trial', 'row'), 'col'), parts along dimension 0, may hold values from -6 to 6
- left_weight: bfloat16 [256, 128], P('trial'), parts along dimension 0, may hold values from -0.5 to 0.5
- right_weight: bfloat16 [256, 128], P('trial'), parts along dimension 0, may hold values from -0.5 to 0.5
- left_gate: bfloat16 [256, 128], P('trial'), parts along dimension 0, may hold values from -0.5 to 0.5
- right_gate: bfloat16 [256, 128], P('trial'), parts along dimension 0, may hold values from -0.5 to 0.5
- mid_gain: float32 [128], replicated, may hold values from 0.25 to 1.75
- out_weight: bfloat16 [256, 128], P('trial'), parts along dimension 0, may hold values from -0.5 to 0.5
- out_gate: bfloat16 [256, 128], P('trial'), parts along dimension 0, may hold values from -0.5 to 0.5
Outputs:
- pair_change: bfloat16 [192, 96, 128], P(('trial', 'row'), 'col'), parts along dimension 0
There are 2 independent parts, one for each index of `trial`. A program takes and returns all parts, laid end to end along the dimension named above; an argument that names none is the same for every part. Nothing has to cross between parts.
All inputs are finite; a program needn't handle non-finite values.
Results may differ from a plain program's by a relative error of at most 0.015.
Values may be sent and summed in bfloat16 or wider, within the bound.
No kernel may reach another device: no remote copies, remote signals or barrier semaphores. Data moves between devices by JAX's collectives and lax.ppermute only.
A program may use at most 64 MiB of HBM per device.

v0:
```python
import jax
import jax.numpy as jnp
from jax import lax
from jax.sharding import PartitionSpec as P


def norm_channels(values, channel_gain):
    centred = values - jnp.mean(values, axis=-1, keepdims=True)
    return (
        centred
        * lax.rsqrt(jnp.mean(centred * centred, axis=-1, keepdims=True) + 1e-05)
        * channel_gain
    )


def both_factors(pair_in, left_weight, right_weight, left_gate, right_gate):
    left = jnp.einsum("ijc,cd->ijd", pair_in, left_weight, preferred_element_type=jnp.float32)
    left = left * jax.nn.sigmoid(
        jnp.einsum("ijc,cd->ijd", pair_in, left_gate, preferred_element_type=jnp.float32)
    )
    right = jnp.einsum("ijc,cd->ijd", pair_in, right_weight, preferred_element_type=jnp.float32)
    right = right * jax.nn.sigmoid(
        jnp.einsum("ijc,cd->ijd", pair_in, right_gate, preferred_element_type=jnp.float32)
    )
    return (pair_in, left.astype(jnp.bfloat16), right.astype(jnp.bfloat16))


def close_update(mixed, ready, mid_gain, out_weight, out_gate):
    scaled = norm_channels(mixed.astype(jnp.float32), mid_gain).astype(jnp.bfloat16)
    scaled = lax.optimization_barrier(scaled)
    gate = jax.nn.sigmoid(
        jnp.einsum("ijc,cd->ijd", ready, out_gate, preferred_element_type=jnp.float32)
    )
    return (
        jnp.einsum("ijd,dc->ijc", scaled, out_weight, preferred_element_type=jnp.float32) * gate
    ).astype(jnp.bfloat16)


def per_device(
    pair_rows, left_weight, right_weight, left_gate, right_gate, mid_gain, out_weight, out_gate
):
    ready, left, right = both_factors(pair_rows, left_weight, right_weight, left_gate, right_gate)
    count = pair_rows.shape[0] * lax.axis_size("row")
    left_lines, right_lines = (
        lax.all_to_all(left, "row", split_axis=2, concat_axis=0, tiled=True),
        lax.all_to_all(right, "row", split_axis=2, concat_axis=0, tiled=True),
    )
    strip = jnp.einsum(
        "kid,kjd->ijd",
        lax.all_gather(left_lines, "col", axis=1, tiled=True),
        right_lines,
        preferred_element_type=jnp.float32,
    )
    strip = (strip * count ** (-0.5)).astype(jnp.bfloat16)
    mixed = lax.all_to_all(strip, "row", split_axis=0, concat_axis=2, tiled=True)
    return close_update(mixed, ready, mid_gain, out_weight, out_gate)


def solution(mesh):
    placed = (
        P(("trial", "row"), "col", None),
        P("trial", None),
        P("trial", None),
        P("trial", None),
        P("trial", None),
        P(),
        P("trial", None),
        P("trial", None),
    )
    return jax.shard_map(
        per_device,
        mesh=mesh,
        in_specs=placed,
        out_specs=P(("trial", "row"), "col", None),
        check_vma=False,
    )
```

profile of v0, /device:TPU:0, one launch (start us, length us, event | category | flops | bytes accessed | tf_op | source)
XLA Modules:
  0.0 60.2 jit_solution(2696725952080728674)
XLA Ops:
  0.0 0.9 %copy-done = bf16[24,24,128]{2,1,0:T(8,128)(2,1)S(1)} copy-done((bf16[24,24,128]{2,1,0:T(8,128)(2,1)S(1)}, bf16[24,24,128]{2,1,0:T(8,128)(2,1)}, u32[]{:S(2)}) %copy-start) | copy-done | bytes 147480
  0.9 1.0 %fusion.6 = f32[24,24,128]{2,1,0:T(8,128)S(1)} fusion(bf16[24,24,128]{2,1,0:T(8,128)(2,1)S(1)} %copy-done, bf16[128,128]{1,0:T(8,128)(2,1)} %param.11), kind=kOutput, calls=%fused_computation.13 | convolution fusion | flops 19095552 | bytes 475136 | tf_op jit(solution)/shard_map/ijc,cd->ijd/dot_general | solution.py:19
  1.9 1.0 %fusion.11 = bf16[24,24,128]{2,1,0:T(8,128)(2,1)S(1)} fusion(f32[24,24,128]{2,1,0:T(8,128)S(1)} %fusion.6, bf16[24,24,128]{2,1,0:T(8,128)(2,1)S(1)} %copy-done, bf16[128,128]{1,0:T(8,128)(2,1)} %param.9), kind=kOutput, calls=%fused_computation.19 | convolution fusion | flops 19021824 | bytes 622592 | tf_op jit(solution)/shard_map/ijc,cd->ijd/dot_general | solution.py:17
  2.9 0.4 copy.52
  3.4 1.7 %reshape.28 = bf16[4,2,9216]{2,1,0:T(2,128)(2,1)} reshape(bf16[128,24,24]{2,1,0:T(8,128)(2,1)S(1)} %bitcast.45) | data formatting | bytes 294912
  5.0 5.2 %all-to-all-start.1 = ((bf16[4,2,9216]{2,1,0:T(2,128)(2,1)}), bf16[4,2,9216]{2,1,0:T(2,128)(2,1)S(1)}, u32[]{:S(2)}, u32[]{:S(2)}) async-start(bf16[4,2,9216]{2,1,0:T(2,128)(2,1)} %reshape.28), calls=%async_computation.1 | async-start | bytes 294912 | tf_op jit(solution)/shard_map/all_to_all | solution.py:45
  10.7 0.4 copy.50
  11.1 1.6 %reshape.30 = bf16[4,2,9216]{2,1,0:T(2,128)(2,1)} reshape(bf16[128,24,24]{2,1,0:T(8,128)(2,1)S(1)} %bitcast.46) | data formatting | bytes 294912
  12.8 2.5 %all-to-all-done.1 = bf16[4,2,9216]{2,1,0:T(2,128)(2,1)S(1)} async-done(((bf16[4,2,9216]{2,1,0:T(2,128)(2,1)}), bf16[4,2,9216]{2,1,0:T(2,128)(2,1)S(1)}, u32[]{:S(2)}, u32[]{:S(2)}) %all-to-all-start.1) | async-done | bytes 147488 | tf_op jit(solution)/shard_map/all_to_all | solution.py:45
  15.3 3.3 %all-to-all-start = ((bf16[4,2,9216]{2,1,0:T(2,128)(2,1)}), bf16[4,2,9216]{2,1,0:T(2,128)(2,1)S(1)}, u32[]{:S(2)}, u32[]{:S(2)}) async-start(bf16[4,2,9216]{2,1,0:T(2,128)(2,1)} %reshape.30), calls=%async_computation | async-start | bytes 294912 | tf_op jit(solution)/shard_map/all_to_all | solution.py:46
  18.6 1.1 %reshape.29 = bf16[128,24,24]{2,1,0:T(8,128)(2,1)S(1)} reshape(bf16[4,2,9216]{2,1,0:T(2,128)(2,1)S(1)} %all-to-all-done.1) | data formatting | bytes 294912
  19.7 1.5 %copy.53 = bf16[24,24,4,32]{0,2,3,1:T(4,128)(2,1)S(1)} copy(bf16[24,24,4,32]{1,0,3,2:T(8,128)(2,1)S(1)} %bitcast.47) | data formatting | bytes 294912 | tf_op jit(solution)/shard_map/all_to_all | solution.py:45
  21.7 19.5 %all_gather.3 = bf16[96,96,32]{0,1,2:T(8,128)(2,1)S(1)} all-gather(bf16[96,24,32]{0,1,2:T(8,128)(2,1)S(1)} %copy.54), channel_id=1, replica_groups=mesh['row'=4,'col'=4,'trial'=2] {'col'}, dimensions={1}, use_global_device_ids=true | all-gather | bytes 737280 | tf_op jit(solution)/shard_map/all_gather | solution.py:50
  41.2 1.1 %reshape.31 = bf16[128,24,24]{2,1,0:T(8,128)(2,1)S(1)} reshape(bf16[4,2,9216]{2,1,0:T(2,128)(2,1)S(1)} %all-to-all-done) | data formatting | bytes 294912
  42.3 1.5 %copy.51 = bf16[24,24,4,32]{0,2,3,1:T(4,128)(2,1)S(1)} copy(bf16[24,24,4,32]{1,0,3,2:T(8,128)(2,1)S(1)} %bitcast.48) | data formatting | bytes 294912 | tf_op jit(solution)/shard_map/all_to_all | solution.py:46
  44.2 0.5 fusion.13
  45.1 1.2 %reshape.32 = bf16[4,2,9216]{2,1,0:T(2,128)(2,1)} reshape(bf16[96,24,32]{2,1,0:T(8,128)(2,1)S(1)} %copy.56) | data formatting | bytes 294912
  46.3 3.9 %all-to-all-start.2 = ((bf16[4,2,9216]{2,1,0:T(2,128)(2,1)}), bf16[4,2,9216]{2,1,0:T(2,128)(2,1)S(1)}, u32[]{:S(2)}, u32[]{:S(2)}) async-start(bf16[4,2,9216]{2,1,0:T(2,128)(2,1)} %reshape.32), calls=%async_computation.2 | async-start | bytes 294912 | tf_op jit(solution)/shard_map/all_to_all | solution.py:55
  50.5 4.8 %all-to-all-done.2 = bf16[4,2,9216]{2,1,0:T(2,128)(2,1)S(1)} async-done(((bf16[4,2,9216]{2,1,0:T(2,128)(2,1)}), bf16[4,2,9216]{2,1,0:T(2,128)(2,1)S(1)}, u32[]{:S(2)}, u32[]{:S(2)}) %all-to-all-start.2) | async-done | bytes 147488 | tf_op jit(solution)/shard_map/all_to_all | solution.py:55
  55.9 0.7 %reshape.21 = f32[4,24,24,32]{1,0,3,2:T(4,128)S(1)} reshape(bf16[96,24,32]{0,2,1:T(8,128)(2,1)S(1)} %copy.57) | data formatting | bytes 442368 | tf_op jit(solution)/shard_map/convert_element_type | solution.py:29
  56.9 0.5 multiply_reduce_fusion
  57.5 1.0 %copy.58 = f32[24,24,4,32]{3,2,1,0:T(4,128)S(1)} copy(f32[24,24,4,32]{0,2,3,1:T(4,128)S(1)} %bitcast.44) | data formatting | bytes 589824 | tf_op jit(solution)/shard_map/convert_element_type | solution.py:29
  58.6 0.5 reshape.19
  59.4 0.9 %fusion.12 = bf16[24,24,128]{2,1,0:T(8,128)(2,1)} fusion(f32[24,24,128]{2,1,0:T(8,128)S(1)} %fusion.3, bf16[24,24,128]{2,1,0:T(8,128)(2,1)S(1)} %multiply_convert_fusion, bf16[128,128]{1,0:T(8,128)(2,1)S(1)} %copy-done.2), kind=kOutput, calls=%fused_computation.20 | convolution fusion | flops 19021824 | bytes 622592 | tf_op jit(solution)/shard_map/ijd,dc->ijc/dot_general | solution.py:35
  (27 shorter events, 3.3 us)
Async XLA Ops:
  0.0 0.9 %copy-start = (bf16[24,24,128]{2,1,0:T(8,128)(2,1)S(1)}, bf16[24,24,128]{2,1,0:T(8,128)(2,1)}, u32[]{:S(2)}) copy-start(bf16[24,24,128]{2,1,0:T(8,128)(2,1)} %param.8) | copy-start | bytes 442372
  1.9 8.3 %copy-start.4 = (bf16[128,128]{1,0:T(8,128)(2,1)S(1)}, bf16[128,128]{1,0:T(8,128)(2,1)}, u32[]{:S(2)}) copy-start(bf16[128,128]{1,0:T(8,128)(2,1)} %param.12) | copy-start | bytes 98308
  2.9 7.5 %copy-start.1 = (bf16[128,128]{1,0:T(8,128)(2,1)S(1)}, bf16[128,128]{1,0:T(8,128)(2,1)}, u32[]{:S(2)}) copy-start(bf16[128,128]{1,0:T(8,128)(2,1)} %param.10) | copy-start | bytes 98308
  5.0 10.3 %all-to-all-start.1 = ((bf16[4,2,9216]{2,1,0:T(2,128)(2,1)}), bf16[4,2,9216]{2,1,0:T(2,128)(2,1)S(1)}, u32[]{:S(2)}, u32[]{:S(2)}) async-start(bf16[4,2,9216]{2,1,0:T(2,128)(2,1)} %reshape.28), calls=%async_computation.1 | async-start | bytes 294912 | tf_op jit(solution)/shard_map/all_to_all | solution.py:45
  15.3 25.9 %all-to-all-start = ((bf16[4,2,9216]{2,1,0:T(2,128)(2,1)}), bf16[4,2,9216]{2,1,0:T(2,128)(2,1)S(1)}, u32[]{:S(2)}, u32[]{:S(2)}) async-start(bf16[4,2,9216]{2,1,0:T(2,128)(2,1)} %reshape.30), calls=%async_computation | async-start | bytes 294912 | tf_op jit(solution)/shard_map/all_to_all | solution.py:46
  44.1 6.1 %copy-start.5 = (bf16[128,128]{1,0:T(8,128)(2,1)S(1)}, bf16[128,128]{1,0:T(8,128)(2,1)}, u32[]{:S(2)}) copy-start(bf16[128,128]{1,0:T(8,128)(2,1)} %param.15) | copy-start | bytes 98308
  46.3 9.0 %all-to-all-start.2 = ((bf16[4,2,9216]{2,1,0:T(2,128)(2,1)}), bf16[4,2,9216]{2,1,0:T(2,128)(2,1)S(1)}, u32[]{:S(2)}, u32[]{:S(2)}) async-start(bf16[4,2,9216]{2,1,0:T(2,128)(2,1)} %reshape.32), calls=%async_computation.2 | async-start | bytes 294912 | tf_op jit(solution)/shard_map/all_to_all | solution.py:55
  57.5 1.6 %copy-start.3 = (f32[128]{0:T(128)S(1)}, f32[128]{0:T(128)}, u32[]{:S(2)}) copy-start(f32[128]{0:T(128)} %param.13) | copy-start | bytes 1540
  58.6 0.8 %copy-start.2 = (bf16[128,128]{1,0:T(8,128)(2,1)S(1)}, bf16[128,128]{1,0:T(8,128)(2,1)}, u32[]{:S(2)}) copy-start(bf16[128,128]{1,0:T(8,128)(2,1)} %param.14) | copy-start | bytes 98308
where the time goes:
time: 60.9 us; the launch traced here: 60.2 us
  blocking collectives  19.5 us (32%)
  local copies, waits for them, and re-layouts  15.7 us (26%)
  starting transfers between devices  12.4 us (20%)
  waiting for transfers between devices  7.31 us (12%)
  matrix products  4.11 us (7%)
  other arithmetic  1 us (2%)
    all_gather x1, blocking collectives, per_device(): lax.all_gather(left_lines, 'col', axis=1, tiled=True)  19.5 us
    unnamed x18, local copies, waits for them, and re-layouts  7.92 us
    all_to_all x1, starting transfers between devices, per_device(): lax.all_to_all(left, 'row', split_axis=2, concat_axis=0, tiled=True)  5.19 us
    all_to_all x1, waiting for transfers between devices, per_device(): lax.all_to_all(strip, 'row', split_axis=0, concat_axis=2, tiled=True)  4.81 us
    all_to_all x1, starting transfers between devices, per_device(): lax.all_to_all(strip, 'row', split_axis=0, concat_axis=2, tiled=True)  3.9 us
    all_to_all x1, starting transfers between devices, per_device(): lax.all_to_all(right, 'row', split_axis=2, concat_axis=0, tiled=True)  3.33 us
    all_to_all x1, waiting for transfers between devices, per_device(): lax.all_to_all(left, 'row', split_axis=2, concat_axis=0, tiled=True)  2.49 us
    convert_element_type x3, local copies, waits for them, and re-layouts, close_update(): mixed.astype(jnp.float32)  2.21 us
  transfers between devices with their start and end apart: 3, of which 2 were waited for; matrix products, arithmetic and copies ran while one was open for 9% of the time, Pallas kernels for 0%

commit v1 on v0

v1 whole, which is shorter than its diff:
```python
import functools

import jax
import jax.numpy as jnp
from jax import lax
from jax.experimental import pallas as pl
from jax.experimental.pallas import tpu as pltpu
from jax.sharding import PartitionSpec as P

F32 = jnp.float32
BF16 = jnp.bfloat16
NEAR_BYTES = 4 * 2**20


def logistic(x):
    return 0.5 + 0.5 * jnp.tanh(0.5 * x)


def pick(a, b, n):
    return a ^ b if n & (n - 1) == 0 else (a + b) % n


def factor(x, weight, gate):
    width = weight.shape[1]
    both = jnp.concatenate([weight, gate], axis=1)
    prod = jnp.dot(x, both, preferred_element_type=F32)
    return (prod[:, :width] * logistic(prod[:, width:])).astype(BF16).astype(F32)


def right_kernel(x_ref, weight_ref, gate_ref, out_gate_ref, *refs):
    right_ref, out_ref = refs[-2:]
    rows = right_ref.shape[0]
    me = lax.axis_index("row")
    out_ref[...] = logistic(jnp.dot(x_ref[...], out_gate_ref[...], preferred_element_type=F32))
    for m, each in enumerate((x_ref,) + refs[:-2]):
        right = factor(each[...], weight_ref[...], gate_ref[...])
        right_ref[pick(me, m, rows)] = right.reshape(right_ref.shape[1:])


def add_line(u, x_ref, weight_ref, gate_ref, right_ref, acc_ref, left_f):
    left_f[...] = factor(x_ref[...], weight_ref[...], gate_ref[...]).reshape(left_f.shape)
    k_count, j_count, _ = left_f.shape
    rows, cols = lax.axis_size("row"), lax.axis_size("col")
    e = pick(lax.axis_index("col"), u, cols)
    source = e // (cols // rows)
    base = e % (cols // rows) * j_count
    group, chunk = 4, 8

    def one_group(g, _):
        at = g * group

        def some_k(t, sums):
            sums = list(sums)
            for kk in range(chunk):
                k = t * chunk + kk
                row = right_ref[source, k]
                for ii in range(group):
                    sums[ii] = sums[ii] + left_f[k, pl.ds(at + ii, 1), :] * row
            return tuple(sums)

        sums = tuple(acc_ref[base + at + ii] for ii in range(group))
        sums = lax.fori_loop(0, k_count // chunk, some_k, sums)
        for ii in range(group):
            acc_ref[base + at + ii] = sums[ii]
        return 0

    lax.fori_loop(0, j_count // group, one_group, 0)


def first_kernel(u, x_ref, weight_ref, gate_ref, right_ref, acc_ref, left_f):
    acc_ref[...] = jnp.zeros_like(acc_ref)
    add_line(u, x_ref, weight_ref, gate_ref, right_ref, acc_ref, left_f)


def next_kernel(u, x_ref, weight_ref, gate_ref, right_ref, old_ref, acc_ref, left_f):
    del old_ref
    add_line(u, x_ref, weight_ref, gate_ref, right_ref, acc_ref, left_f)


def last_kernel(
    u, n, x_ref, weight_ref, gate_ref, right_ref, old_ref,
    out_gate_ref, gain_ref, out_weight_ref, out_ref, left_f,
):
    add_line(u, x_ref, weight_ref, gate_ref, right_ref, old_ref, left_f)
    mixed = (old_ref[...] * n ** (-0.5)).astype(BF16).astype(F32)
    centred = mixed - jnp.mean(mixed, axis=-1, keepdims=True)
    var = jnp.mean(centred * centred, axis=-1, keepdims=True)
    scaled = centred * lax.rsqrt(var + 1e-05) * gain_ref[...]
    scaled = scaled.reshape(-1, scaled.shape[-1]).astype(BF16)
    prod = jnp.dot(scaled, out_weight_ref[...], preferred_element_type=F32)
    out_ref[...] = (prod * out_gate_ref[...]).astype(out_ref.dtype)


VMEM = pl.BlockSpec(memory_space=pltpu.VMEM)


def call(kernel, near, outs, scratch, *args, aliases={}):
    if near:
        args = [pltpu.with_memory_space_constraint(each, pltpu.VMEM) for each in args]
    return pl.pallas_call(
        kernel,
        out_shape=outs,
        in_specs=[VMEM] * len(args),
        out_specs=jax.tree.map(lambda _: VMEM, outs),
        input_output_aliases=aliases,
        scratch_shapes=[pltpu.VMEM(each, F32) for each in scratch],
    )(*args)


def update(
    pair_rows, left_weight, right_weight, left_gate, right_gate, mid_gain, out_weight, out_gate
):
    k_count, j_count, width = pair_rows.shape
    mix = left_weight.shape[1]
    rows, cols = lax.axis_size("row"), lax.axis_size("col")
    n = k_count * rows
    per_row = cols // rows
    flat = pair_rows.reshape(k_count * j_count, width)
    block = (k_count, j_count, mix)
    rights = []
    for m in range(1, rows):
        rights.append(lax.ppermute(flat, "row", [(pick(s, m, rows), s) for s in range(rows)]))
    lefts = []
    for u in range(cols):
        moves = []
        for rr in range(rows):
            for cc in range(cols):
                e = pick(cc, u, cols)
                moves.append((e // per_row * cols + rr * per_row + e % per_row, rr * cols + cc))
        lefts.append(lax.ppermute(flat, ("row", "col"), moves))
    one = k_count * j_count * max(mix, width)
    near = one * (4 * (rows + 2) + 2 * (rows + cols)) <= NEAR_BYTES
    held = pltpu.VMEM if near else jax.ShapeDtypeStruct
    right, gate = call(
        right_kernel,
        near,
        (held((rows,) + block, F32), held((k_count * j_count, width), F32)),
        [], flat, right_weight, right_gate, out_gate, *rights,
    )
    total = None
    for u in range(cols):
        args = [lefts[u], left_weight, left_gate, right]
        if u == 0:
            total = call(functools.partial(first_kernel, u), near, held(block, F32), [block], *args)
        elif u < cols - 1:
            total = call(
                functools.partial(next_kernel, u), near, held(block, F32), [block],
                *args, total, aliases={4: 0},
            )
        else:
            out = call(
                functools.partial(last_kernel, u, n), near,
                jax.ShapeDtypeStruct(flat.shape, BF16), [block],
                *args, total, gate, mid_gain.reshape(1, -1), out_weight,
            )
    return out.reshape(pair_rows.shape)


def solution(mesh):
    placed = (
        P(("trial", "row"), "col", None),
        P("trial", None),
        P("trial", None),
        P("trial", None),
        P("trial", None),
        P(),
        P("trial", None),
        P("trial", None),
    )
    return jax.shard_map(
        update,
        mesh=mesh,
        in_specs=placed,
        out_specs=P(("trial", "row"), "col", None),
        check_vma=False,
    )
```

time: 60.9 us -> 28.1 us (0.46)
  the two profiles are of different devices: /device:TPU:0 before, /device:TPU:4 now
where the time goes in v1:
time: 28.1 us; the launch traced here: 27.6 us
  starting transfers between devices  12.6 us (45%)
  waiting for transfers between devices  5.29 us (19%)
  Pallas kernels  4.93 us (18%)
  local copies, waits for them, and re-layouts  4.75 us (17%)
    ppermute x4, starting transfers between devices, update(): lefts.append(lax.ppermute(flat, ('row', 'col'), moves))  9.07 us
    pallas_call x5, Pallas kernels, call(): pl.pallas_call(kernel, out_shape=outs, in_specs=[VMEM] * len(args), out_s...  4.93 us
    unnamed x20, local copies, waits for them, and re-layouts  4.75 us
    ppermute x4, waiting for transfers between devices, update(): lefts.append(lax.ppermute(flat, ('row', 'col'), moves))  4.59 us
    ppermute x3, starting transfers between devices, update(): lax.ppermute(flat, 'row', [(pick(s, m, rows), s) for s in range(rows)])  3.49 us
    ppermute x3, waiting for transfers between devices, update(): lax.ppermute(flat, 'row', [(pick(s, m, rows), s) for s in range(rows)])  0.71 us
  transfers between devices with their start and end apart: 7, of which 3 were waited for; matrix products, arithmetic and copies ran while one was open for 0% of the time, Pallas kernels for 11%

profile of v1, /device:TPU:4, one launch (start us, length us, event | category | flops | bytes accessed | tf_op | source)
XLA Modules:
  0.0 27.6 jit_solution(11147810472820326844)
XLA Ops:
  0.0 1.5 %collective-permute-start.1 = (bf16[576,128]{1,0:T(8,128)(2,1)}, bf16[576,128]{1,0:T(8,128)(2,1)S(1)}, u32[]{:S(2)}, u32[]{:S(2)}) collective-permute-start(bf16[576,128]{1,0:T(8,128)(2,1)} %bitcast.3), channel_id=1, source_target_pairs={{8,0},{0,8},{24,16},{16,24},{9,1},{1,9},{25,17},{17,25},{10,2},{2,... | collective-permute-start | bytes 442376 | tf_op jit(solution)/shard_map/ppermute | solution.py:122
  1.5 0.5 %collective-permute-start.2 = (bf16[576,128]{1,0:T(8,128)(2,1)}, bf16[576,128]{1,0:T(8,128)(2,1)S(1)}, u32[]{:S(2)}, u32[]{:S(2)}) collective-permute-start(bf16[576,128]{1,0:T(8,128)(2,1)} %bitcast.4), channel_id=1, source_target_pairs={{16,0},{24,8},{0,16},{8,24},{17,1},{25,9},{1,17},{9,25},{18,2},{26... | collective-permute-start | bytes 442376 | tf_op jit(solution)/shard_map/ppermute | solution.py:122
  2.0 1.5 %collective-permute-start.3 = (bf16[576,128]{1,0:T(8,128)(2,1)}, bf16[576,128]{1,0:T(8,128)(2,1)S(1)}, u32[]{:S(2)}, u32[]{:S(2)}) collective-permute-start(bf16[576,128]{1,0:T(8,128)(2,1)} %bitcast.5), channel_id=1, source_target_pairs={{24,0},{16,8},{8,16},{0,24},{25,1},{17,9},{9,17},{1,25},{26,2},{18... | collective-permute-start | bytes 442376 | tf_op jit(solution)/shard_map/ppermute | solution.py:122
  3.5 4.4 %collective-permute-start.6 = (bf16[576,128]{1,0:T(8,128)(2,1)}, bf16[576,128]{1,0:T(8,128)(2,1)S(1)}, u32[]{:S(2)}, u32[]{:S(2)}) collective-permute-start(bf16[576,128]{1,0:T(8,128)(2,1)} %bitcast.6), channel_id=1, source_target_pairs={{0,0},{8,2},{16,4},{24,6},{2,8},{10,10},{18,12},{26,14},{4,16},{12... | collective-permute-start | bytes 442376 | tf_op jit(solution)/shard_map/ppermute | solution.py:130
  7.9 3.2 %collective-permute-start.5 = (bf16[576,128]{1,0:T(8,128)(2,1)}, bf16[576,128]{1,0:T(8,128)(2,1)S(1)}, u32[]{:S(2)}, u32[]{:S(2)}) collective-permute-start(bf16[576,128]{1,0:T(8,128)(2,1)} %bitcast.7), channel_id=1, source_target_pairs={{8,0},{0,2},{24,4},{16,6},{10,8},{2,10},{26,12},{18,14},{12,16},{4... | collective-permute-start | bytes 442376 | tf_op jit(solution)/shard_map/ppermute | solution.py:130
  11.1 0.7 %collective-permute-done.2.refs_1_ = bf16[576,128]{1,0:T(8,128)(2,1)S(1)} collective-permute-done((bf16[576,128]{1,0:T(8,128)(2,1)}, bf16[576,128]{1,0:T(8,128)(2,1)S(1)}, u32[]{:S(2)}, u32[]{:S(2)}) %collective-permute-start.2) | collective-permute-done | bytes 147488 | tf_op jit(solution)/shard_map/ppermute | solution.py:122
  11.8 1.5 %collective-permute-start = (bf16[576,128]{1,0:T(8,128)(2,1)}, bf16[576,128]{1,0:T(8,128)(2,1)S(1)}, u32[]{:S(2)}, u32[]{:S(2)}) collective-permute-start(bf16[576,128]{1,0:T(8,128)(2,1)} %bitcast.9), channel_id=1, source_target_pairs={{24,0},{16,2},{8,4},{0,6},{26,8},{18,10},{10,12},{2,14},{28,16},{2... | collective-permute-start | bytes 442376 | tf_op jit(solution)/shard_map/ppermute | solution.py:130
  13.3 0.9 %copy-done.4 = bf16[24,24,128]{2,1,0:T(8,128)(2,1)S(1)} copy-done((bf16[24,24,128]{2,1,0:T(8,128)(2,1)S(1)}, bf16[24,24,128]{2,1,0:T(8,128)(2,1)}, u32[]{:S(2)}) %copy-start.4) | copy-done | bytes 147480
  14.2 0.8 %copy-done.6 = bf16[128,128]{1,0:T(8,128)(2,1)S(1)} copy-done((bf16[128,128]{1,0:T(8,128)(2,1)S(1)}, bf16[128,128]{1,0:T(8,128)(2,1)}, u32[]{:S(2)}) %copy-start.6) | copy-done | bytes 32792
  15.0 0.8 %copy-done.7 = bf16[128,128]{1,0:T(8,128)(2,1)S(1)} copy-done((bf16[128,128]{1,0:T(8,128)(2,1)S(1)}, bf16[128,128]{1,0:T(8,128)(2,1)}, u32[]{:S(2)}) %copy-start.7) | copy-done | bytes 32792
  15.7 0.8 %copy-done.8 = bf16[128,128]{1,0:T(8,128)(2,1)S(1)} copy-done((bf16[128,128]{1,0:T(8,128)(2,1)S(1)}, bf16[128,128]{1,0:T(8,128)(2,1)}, u32[]{:S(2)}) %copy-start.8) | copy-done | bytes 32792
  16.5 0.5 %shard_map.82 = (f32[4,24,24,128]{3,2,1,0:T(8,128)S(1)}, f32[576,128]{1,0:T(8,128)S(1)}) custom-call(bf16[576,128]{1,0:T(8,128)(2,1)S(1)} %bitcast.10, bf16[128,128]{1,0:T(8,128)(2,1)S(1)} %copy-done.6, bf16[128,128]{1,0:T(8,128)(2,1)S(1)} %copy-done.7, bf16[128,128]{1,0:T(8,128)(2,1)S(1)} %copy-done.8, bf16[576,128]{1,0:T(8,128)(2,1)S(1)} %collective-permute-done.1.refs_0_, ...), custom_call_target="tpu_custom_call" | custom-call | tf_op jit(solution)/shard_map/pallas_call | solution.py:100
  17.0 3.2 %collective-permute-done.6.x_ref = bf16[576,128]{1,0:T(8,128)(2,1)S(1)} collective-permute-done((bf16[576,128]{1,0:T(8,128)(2,1)}, bf16[576,128]{1,0:T(8,128)(2,1)S(1)}, u32[]{:S(2)}, u32[]{:S(2)}) %collective-permute-start.6) | collective-permute-done | bytes 147488 | tf_op jit(solution)/shard_map/ppermute | solution.py:130
  20.2 0.8 %copy-done = bf16[128,128]{1,0:T(8,128)(2,1)S(1)} copy-done((bf16[128,128]{1,0:T(8,128)(2,1)S(1)}, bf16[128,128]{1,0:T(8,128)(2,1)}, u32[]{:S(2)}) %copy-start) | copy-done | bytes 32792
  21.0 0.8 %copy-done.2 = bf16[128,128]{1,0:T(8,128)(2,1)S(1)} copy-done((bf16[128,128]{1,0:T(8,128)(2,1)S(1)}, bf16[128,128]{1,0:T(8,128)(2,1)}, u32[]{:S(2)}) %copy-start.2) | copy-done | bytes 32792
  21.8 0.8 %shard_map.83.old_ref = f32[24,24,128]{2,1,0:T(8,128)S(1)} custom-call(bf16[576,128]{1,0:T(8,128)(2,1)S(1)} %collective-permute-done.6.x_ref, bf16[128,128]{1,0:T(8,128)(2,1)S(1)} %copy-done, bf16[128,128]{1,0:T(8,128)(2,1)S(1)} %copy-done.2, f32[4,24,24,128]{3,2,1,0:T(8,128)S(1)} %get-tuple-element.7.right_ref), custom_call_target="tpu_custom_call" | custom-call | tf_op jit(solution)/shard_map/pallas_call | solution.py:100
  22.6 0.0 collective-permute-done.5.x_ref
  22.6 0.8 %shard_map.84.old_ref = f32[24,24,128]{2,1,0:T(8,128)S(1)} custom-call(bf16[576,128]{1,0:T(8,128)(2,1)S(1)} %collective-permute-done.5.x_ref, bf16[128,128]{1,0:T(8,128)(2,1)S(1)} %copy-done, bf16[128,128]{1,0:T(8,128)(2,1)S(1)} %copy-done.2, f32[4,24,24,128]{3,2,1,0:T(8,128)S(1)} %get-tuple-element.7.right_ref, ...), custom_call_target="tpu_custom_call", output_to_operand_aliasing={{}: (4, {})} | custom-call | tf_op jit(solution)/shard_map/pallas_call | solution.py:100
  23.4 0.0 copy-start.1
  23.5 0.0 copy-start.5
  23.5 0.0 copy-start.9
  23.5 0.8 %shard_map.85.old_ref = f32[24,24,128]{2,1,0:T(8,128)S(1)} custom-call(bf16[576,128]{1,0:T(8,128)(2,1)S(1)} %collective-permute-done.4.x_ref, bf16[128,128]{1,0:T(8,128)(2,1)S(1)} %copy-done, bf16[128,128]{1,0:T(8,128)(2,1)S(1)} %copy-done.2, f32[4,24,24,128]{3,2,1,0:T(8,128)S(1)} %get-tuple-element.7.right_ref, ...), custom_call_target="tpu_custom_call", output_to_operand_aliasing={{}: (4, {})} | custom-call | tf_op jit(solution)/shard_map/pallas_call | solution.py:100
  24.3 1.3 %collective-permute-done.x_ref = bf16[576,128]{1,0:T(8,128)(2,1)S(1)} collective-permute-done((bf16[576,128]{1,0:T(8,128)(2,1)}, bf16[576,128]{1,0:T(8,128)(2,1)S(1)}, u32[]{:S(2)}, u32[]{:S(2)}) %collective-permute-start) | collective-permute-done | bytes 147488 | tf_op jit(solution)/shard_map/ppermute | solution.py:130
  25.7 1.9 %shard_map.86 = bf16[576,128]{1,0:T(8,128)(2,1)} custom-call(bf16[576,128]{1,0:T(8,128)(2,1)S(1)} %collective-permute-done.x_ref, bf16[128,128]{1,0:T(8,128)(2,1)S(1)} %copy-done.1, bf16[128,128]{1,0:T(8,128)(2,1)S(1)} %copy-done.3, f32[4,24,24,128]{3,2,1,0:T(8,128)S(1)} %get-tuple-element.7.right_ref, f32[24,24,128]{2,1,0:T(8,128)S(1)} %shard_map.85.old_ref, ...), custom_call_target="tpu_custom_call" | custom-call | tf_op jit(solution)/shard_map/pallas_call | solution.py:100
  (15 shorter events, 0.0 us)
Async XLA Ops:
  0.0 11.1 %collective-permute-start.1 = (bf16[576,128]{1,0:T(8,128)(2,1)}, bf16[576,128]{1,0:T(8,128)(2,1)S(1)}, u32[]{:S(2)}, u32[]{:S(2)}) collective-permute-start(bf16[576,128]{1,0:T(8,128)(2,1)} %bitcast.3), channel_id=1, source_target_pairs={{8,0},{0,8},{24,16},{16,24},{9,1},{1,9},{25,17},{17,25},{10,2},{2,... | collective-permute-start | bytes 442376 | tf_op jit(solution)/shard_map/ppermute | solution.py:122
  1.5 10.3 %collective-permute-start.2 = (bf16[576,128]{1,0:T(8,128)(2,1)}, bf16[576,128]{1,0:T(8,128)(2,1)S(1)}, u32[]{:S(2)}, u32[]{:S(2)}) collective-permute-start(bf16[576,128]{1,0:T(8,128)(2,1)} %bitcast.4), channel_id=1, source_target_pairs={{16,0},{24,8},{0,16},{8,24},{17,1},{25,9},{1,17},{9,25},{18,2},{26... | collective-permute-start | bytes 442376 | tf_op jit(solution)/shard_map/ppermute | solution.py:122
  2.0 11.3 %collective-permute-start.3 = (bf16[576,128]{1,0:T(8,128)(2,1)}, bf16[576,128]{1,0:T(8,128)(2,1)S(1)}, u32[]{:S(2)}, u32[]{:S(2)}) collective-permute-start(bf16[576,128]{1,0:T(8,128)(2,1)} %bitcast.5), channel_id=1, source_target_pairs={{24,0},{16,8},{8,16},{0,24},{25,1},{17,9},{9,17},{1,25},{26,2},{18... | collective-permute-start | bytes 442376 | tf_op jit(solution)/shard_map/ppermute | solution.py:122
  3.5 16.8 %collective-permute-start.6 = (bf16[576,128]{1,0:T(8,128)(2,1)}, bf16[576,128]{1,0:T(8,128)(2,1)S(1)}, u32[]{:S(2)}, u32[]{:S(2)}) collective-permute-start(bf16[576,128]{1,0:T(8,128)(2,1)} %bitcast.6), channel_id=1, source_target_pairs={{0,0},{8,2},{16,4},{24,6},{2,8},{10,10},{18,12},{26,14},{4,16},{12... | collective-permute-start | bytes 442376 | tf_op jit(solution)/shard_map/ppermute | solution.py:130
  7.9 14.7 %collective-permute-start.5 = (bf16[576,128]{1,0:T(8,128)(2,1)}, bf16[576,128]{1,0:T(8,128)(2,1)S(1)}, u32[]{:S(2)}, u32[]{:S(2)}) collective-permute-start(bf16[576,128]{1,0:T(8,128)(2,1)} %bitcast.7), channel_id=1, source_target_pairs={{8,0},{0,2},{24,4},{16,6},{10,8},{2,10},{26,12},{18,14},{12,16},{4... | collective-permute-start | bytes 442376 | tf_op jit(solution)/shard_map/ppermute | solution.py:130
  11.1 12.4 %collective-permute-start.4 = (bf16[576,128]{1,0:T(8,128)(2,1)}, bf16[576,128]{1,0:T(8,128)(2,1)S(1)}, u32[]{:S(2)}, u32[]{:S(2)}) collective-permute-start(bf16[576,128]{1,0:T(8,128)(2,1)} %bitcast.8), channel_id=1, source_target_pairs={{16,0},{24,2},{0,4},{8,6},{18,8},{26,10},{2,12},{10,14},{20,16},{2... | collective-permute-start | bytes 442376 | tf_op jit(solution)/shard_map/ppermute | solution.py:130
  11.8 13.9 %collective-permute-start = (bf16[576,128]{1,0:T(8,128)(2,1)}, bf16[576,128]{1,0:T(8,128)(2,1)S(1)}, u32[]{:S(2)}, u32[]{:S(2)}) collective-permute-start(bf16[576,128]{1,0:T(8,128)(2,1)} %bitcast.9), channel_id=1, source_target_pairs={{24,0},{16,2},{8,4},{0,6},{26,8},{18,10},{10,12},{2,14},{28,16},{2... | collective-permute-start | bytes 442376 | tf_op jit(solution)/shard_map/ppermute | solution.py:130
  13.3 0.9 %copy-start.4 = (bf16[24,24,128]{2,1,0:T(8,128)(2,1)S(1)}, bf16[24,24,128]{2,1,0:T(8,128)(2,1)}, u32[]{:S(2)}) copy-start(bf16[24,24,128]{2,1,0:T(8,128)(2,1)} %param.8) | copy-start | bytes 442372
  14.2 0.8 %copy-start.6 = (bf16[128,128]{1,0:T(8,128)(2,1)S(1)}, bf16[128,128]{1,0:T(8,128)(2,1)}, u32[]{:S(2)}) copy-start(bf16[128,128]{1,0:T(8,128)(2,1)} %weight_ref.5) | copy-start | bytes 98308
  15.0 0.8 %copy-start.7 = (bf16[128,128]{1,0:T(8,128)(2,1)S(1)}, bf16[128,128]{1,0:T(8,128)(2,1)}, u32[]{:S(2)}) copy-start(bf16[128,128]{1,0:T(8,128)(2,1)} %gate_ref.5) | copy-start | bytes 98308
  15.7 0.8 %copy-start.8 = (bf16[128,128]{1,0:T(8,128)(2,1)S(1)}, bf16[128,128]{1,0:T(8,128)(2,1)}, u32[]{:S(2)}) copy-start(bf16[128,128]{1,0:T(8,128)(2,1)} %out_gate_ref.1) | copy-start | bytes 98308
  20.2 0.8 %copy-start = (bf16[128,128]{1,0:T(8,128)(2,1)S(1)}, bf16[128,128]{1,0:T(8,128)(2,1)}, u32[]{:S(2)}) copy-start(bf16[128,128]{1,0:T(8,128)(2,1)} %weight_ref.9) | copy-start | bytes 98308
  21.0 0.8 %copy-start.2 = (bf16[128,128]{1,0:T(8,128)(2,1)S(1)}, bf16[128,128]{1,0:T(8,128)(2,1)}, u32[]{:S(2)}) copy-start(bf16[128,128]{1,0:T(8,128)(2,1)} %gate_ref.9) | copy-start | bytes 98308
  23.4 2.2 %copy-start.1 = (bf16[128,128]{1,0:T(8,128)(2,1)S(1)}, bf16[128,128]{1,0:T(8,128)(2,1)}, u32[]{:S(2)}) copy-start(bf16[128,128]{1,0:T(8,128)(2,1)} %weight_ref.9) | copy-start | bytes 98308
  23.5 2.2 %copy-start.3 = (bf16[128,128]{1,0:T(8,128)(2,1)S(1)}, bf16[128,128]{1,0:T(8,128)(2,1)}, u32[]{:S(2)}) copy-start(bf16[128,128]{1,0:T(8,128)(2,1)} %gate_ref.9) | copy-start | bytes 98308
  23.5 2.2 %copy-start.5 = (bf16[128,128]{1,0:T(8,128)(2,1)S(1)}, bf16[128,128]{1,0:T(8,128)(2,1)}, u32[]{:S(2)}) copy-start(bf16[128,128]{1,0:T(8,128)(2,1)} %out_weight_ref.1) | copy-start | bytes 98308
  23.5 2.2 %copy-start.9 = (f32[128]{0:T(128)S(1)}, f32[128]{0:T(128)}, u32[]{:S(2)}) copy-start(f32[128]{0:T(128)} %param.13) | copy-start | bytes 1540

commit v2 on v1

--- a/solution.py
+++ b/solution.py
@@ -20,25 +20,35 @@
     return a ^ b if n & (n - 1) == 0 else (a + b) % n
 
 
-def factor(x, weight, gate):
-    width = weight.shape[1]
-    both = jnp.concatenate([weight, gate], axis=1)
+def step_order(rows, cols):
+    half = cols // 2
+    rights = [*range(rows - 1, 0, -1)]
+    lefts = [*range(half, -1, -1), *range(half + 1, cols)]
+    return rights, lefts
+
+
+def factor(x, both):
+    width = both.shape[1] // 2
     prod = jnp.dot(x, both, preferred_element_type=F32)
     return (prod[:, :width] * logistic(prod[:, width:])).astype(BF16).astype(F32)
 
 
-def right_kernel(x_ref, weight_ref, gate_ref, out_gate_ref, *refs):
-    right_ref, out_ref = refs[-2:]
+def right_kernel(
+    x_ref, weight_ref, gate_ref, left_weight_ref, left_gate_ref, out_gate_ref, *refs
+):
+    right_ref, out_ref, left_both_ref = refs[-3:]
     rows = right_ref.shape[0]
     me = lax.axis_index("row")
     out_ref[...] = logistic(jnp.dot(x_ref[...], out_gate_ref[...], preferred_element_type=F32))
-    for m, each in enumerate((x_ref,) + refs[:-2]):
-        right = factor(each[...], weight_ref[...], gate_ref[...])
+    left_both_ref[...] = jnp.concatenate([left_weight_ref[...], left_gate_ref[...]], axis=1)
+    both = jnp.concatenate([weight_ref[...], gate_ref[...]], axis=1)
+    for m, each in enumerate((x_ref,) + refs[:-3]):
+        right = factor(each[...], both)
         right_ref[pick(me, m, rows)] = right.reshape(right_ref.shape[1:])
 
 
-def add_line(u, x_ref, weight_ref, gate_ref, right_ref, acc_ref, left_f):
-    left_f[...] = factor(x_ref[...], weight_ref[...], gate_ref[...]).reshape(left_f.shape)
+def add_line(u, x_ref, both_ref, right_ref, acc_ref, left_f):
+    left_f[...] = factor(x_ref[...], both_ref[...]).reshape(left_f.shape)
     k_count, j_count, _ = left_f.shape
     rows, cols = lax.axis_size("row"), lax.axis_size("col")
     e = pick(lax.axis_index("col"), u, cols)
@@ -67,21 +77,21 @@
     lax.fori_loop(0, j_count // group, one_group, 0)
 
 
-def first_kernel(u, x_ref, weight_ref, gate_ref, right_ref, acc_ref, left_f):
+def first_kernel(u, x_ref, both_ref, right_ref, acc_ref, left_f):
     acc_ref[...] = jnp.zeros_like(acc_ref)
-    add_line(u, x_ref, weight_ref, gate_ref, right_ref, acc_ref, left_f)
+    add_line(u, x_ref, both_ref, right_ref, acc_ref, left_f)
 
 
-def next_kernel(u, x_ref, weight_ref, gate_ref, right_ref, old_ref, acc_ref, left_f):
+def next_kernel(u, x_ref, both_ref, right_ref, old_ref, acc_ref, left_f):
     del old_ref
-    add_line(u, x_ref, weight_ref, gate_ref, right_ref, acc_ref, left_f)
+    add_line(u, x_ref, both_ref, right_ref, acc_ref, left_f)
 
 
 def last_kernel(
-    u, n, x_ref, weight_ref, gate_ref, right_ref, old_ref,
+    u, n, x_ref, both_ref, right_ref, old_ref,
     out_gate_ref, gain_ref, out_weight_ref, out_ref, left_f,
 ):
-    add_line(u, x_ref, weight_ref, gate_ref, right_ref, old_ref, left_f)
+    add_line(u, x_ref, both_ref, right_ref, old_ref, left_f)
     mixed = (old_ref[...] * n ** (-0.5)).astype(BF16).astype(F32)
     centred = mixed - jnp.mean(mixed, axis=-1, keepdims=True)
     var = jnp.mean(centred * centred, axis=-1, keepdims=True)
@@ -94,9 +104,11 @@
 VMEM = pl.BlockSpec(memory_space=pltpu.VMEM)
 
 
-def call(kernel, near, outs, scratch, *args, aliases={}):
+def call(kernel, near, outs, scratch, *args, loose=0, aliases={}):
     if near:
-        args = [pltpu.with_memory_space_constraint(each, pltpu.VMEM) for each in args]
+        args = args[:loose] + tuple(
+            pltpu.with_memory_space_constraint(each, pltpu.VMEM) for each in args[loose:]
+        )
     return pl.pallas_call(
         kernel,
         out_shape=outs,
@@ -131,21 +143,23 @@
     one = k_count * j_count * max(mix, width)
     near = one * (4 * (rows + 2) + 2 * (rows + cols)) <= NEAR_BYTES
     held = pltpu.VMEM if near else jax.ShapeDtypeStruct
-    right, gate = call(
+    right, gate, left_both = call(
         right_kernel,
         near,
-        (held((rows,) + block, F32), held((k_count * j_count, width), F32)),
-        [], flat, right_weight, right_gate, out_gate, *rights,
+        (held((rows,) + block, F32), held((k_count * j_count, width), F32),
+         held((width, 2 * mix), BF16)),
+        [], flat, right_weight, right_gate, left_weight, left_gate, out_gate, *rights, loose=6,
     )
     total = None
-    for u in range(cols):
-        args = [lefts[u], left_weight, left_gate, right]
-        if u == 0:
+    _, steps = step_order(rows, cols)
+    for u in steps:
+        args = [lefts[u], left_both, right]
+        if u == steps[0]:
             total = call(functools.partial(first_kernel, u), near, held(block, F32), [block], *args)
-        elif u < cols - 1:
+        elif u != steps[-1]:
             total = call(
                 functools.partial(next_kernel, u), near, held(block, F32), [block],
-                *args, total, aliases={4: 0},
+                *args, total, aliases={3: 0},
             )
         else:
             out = call(

time: 28.1 us -> 25.2 us (0.90)
  the two profiles are of different devices: /device:TPU:4 before, /device:TPU:5 now
where the time goes in v2:
time: 25.2 us; the launch traced here: 25.1 us
  starting transfers between devices  10.2 us (40%)
  waiting for transfers between devices  8.77 us (35%)
  Pallas kernels  5.94 us (24%)
    ppermute x4, waiting for transfers between devices, update(): lefts.append(lax.ppermute(flat, ('row', 'col'), moves))  8.77 us
    ppermute x4, starting transfers between devices, update(): lefts.append(lax.ppermute(flat, ('row', 'col'), moves))  7.58 us
    pallas_call x5, Pallas kernels, call(): pl.pallas_call(kernel, out_shape=outs, in_specs=[VMEM] * len(args), out_s...  5.94 us
    ppermute x3, starting transfers between devices, update(): lax.ppermute(flat, 'row', [(pick(s, m, rows), s) for s in range(rows)])  2.65 us
  transfers between devices with their start and end apart: 7, of which 2 were waited for; matrix products, arithmetic and copies ran while one was open for 0% of the time, Pallas kernels for 16%

profile of v2, /device:TPU:5, one launch (start us, length us, event | category | flops | bytes accessed | tf_op | source)
XLA Modules:
  0.0 25.1 jit_solution(17927735733601709510)
XLA Ops:
  0.0 1.2 %collective-permute-start.1 = (bf16[576,128]{1,0:T(8,128)(2,1)}, bf16[576,128]{1,0:T(8,128)(2,1)S(1)}, u32[]{:S(2)}, u32[]{:S(2)}) collective-permute-start(bf16[576,128]{1,0:T(8,128)(2,1)} %bitcast.4), channel_id=1, source_target_pairs={{8,0},{0,8},{24,16},{16,24},{9,1},{1,9},{25,17},{17,25},{10,2},{2,... | collective-permute-start | bytes 442376 | tf_op jit(solution)/shard_map/ppermute | solution.py:134
  1.2 0.2 collective-permute-start.2
  1.4 1.2 %collective-permute-start.3 = (bf16[576,128]{1,0:T(8,128)(2,1)}, bf16[576,128]{1,0:T(8,128)(2,1)S(1)}, u32[]{:S(2)}, u32[]{:S(2)}) collective-permute-start(bf16[576,128]{1,0:T(8,128)(2,1)} %bitcast.6), channel_id=1, source_target_pairs={{24,0},{16,8},{8,16},{0,24},{25,1},{17,9},{9,17},{1,25},{26,2},{18... | collective-permute-start | bytes 442376 | tf_op jit(solution)/shard_map/ppermute | solution.py:134
  2.6 0.0 collective-permute-start.6
  2.7 5.3 %collective-permute-start.5 = (bf16[576,128]{1,0:T(8,128)(2,1)}, bf16[576,128]{1,0:T(8,128)(2,1)S(1)}, u32[]{:S(2)}, u32[]{:S(2)}) collective-permute-start(bf16[576,128]{1,0:T(8,128)(2,1)} %bitcast.8), channel_id=1, source_target_pairs={{8,0},{0,2},{24,4},{16,6},{10,8},{2,10},{26,12},{18,14},{12,16},{4... | collective-permute-start | bytes 442376 | tf_op jit(solution)/shard_map/ppermute | solution.py:142
  8.0 0.0 collective-permute-done.1.refs_0_
  8.0 1.9 %collective-permute-start.4 = (bf16[576,128]{1,0:T(8,128)(2,1)}, bf16[576,128]{1,0:T(8,128)(2,1)S(1)}, u32[]{:S(2)}, u32[]{:S(2)}) collective-permute-start(bf16[576,128]{1,0:T(8,128)(2,1)} %bitcast.9), channel_id=1, source_target_pairs={{0,0},{8,2},{16,4},{24,6},{2,8},{10,10},{18,12},{26,14},{4,16},{12... | collective-permute-start | bytes 442376 | tf_op jit(solution)/shard_map/ppermute | solution.py:142
  9.9 0.0 collective-permute-done.2.refs_1_
  9.9 0.4 %collective-permute-start = (bf16[576,128]{1,0:T(8,128)(2,1)}, bf16[576,128]{1,0:T(8,128)(2,1)S(1)}, u32[]{:S(2)}, u32[]{:S(2)}) collective-permute-start(bf16[576,128]{1,0:T(8,128)(2,1)} %bitcast.10), channel_id=1, source_target_pairs={{24,0},{16,2},{8,4},{0,6},{26,8},{18,10},{10,12},{2,14},{28,16},{2... | collective-permute-start | bytes 442376 | tf_op jit(solution)/shard_map/ppermute | solution.py:142
  10.3 0.0 collective-permute-done.3.refs_2_
  10.3 1.5 %shard_map.82 = (f32[4,24,24,128]{3,2,1,0:T(8,128)S(1)}, f32[576,128]{1,0:T(8,128)S(1)}, bf16[128,256]{1,0:T(8,128)(2,1)S(1)}) custom-call(bf16[576,128]{1,0:T(8,128)(2,1)} %bitcast.11, bf16[128,128]{1,0:T(8,128)(2,1)} %weight_ref.1, bf16[128,128]{1,0:T(8,128)(2,1)} %gate_ref.1, bf16[128,128]{1,0:T(8,128)(2,1)} %left_weight_ref.1, ...), custom_call_target="tpu_custom_call" | custom-call | tf_op jit(solution)/shard_map/pallas_call | solution.py:112
  11.8 0.0 collective-permute-done.6.x_ref
  11.8 0.8 %shard_map.83.old_ref = f32[24,24,128]{2,1,0:T(8,128)S(1)} custom-call(bf16[576,128]{1,0:T(8,128)(2,1)S(1)} %collective-permute-done.6.x_ref, bf16[128,256]{1,0:T(8,128)(2,1)S(1)} %get-tuple-element.8.both_ref, f32[4,24,24,128]{3,2,1,0:T(8,128)S(1)} %get-tuple-element.9.right_ref), custom_call_target="tpu_custom_call" | custom-call | tf_op jit(solution)/shard_map/pallas_call | solution.py:112
  12.6 3.9 %collective-permute-done.5.x_ref = bf16[576,128]{1,0:T(8,128)(2,1)S(1)} collective-permute-done((bf16[576,128]{1,0:T(8,128)(2,1)}, bf16[576,128]{1,0:T(8,128)(2,1)S(1)}, u32[]{:S(2)}, u32[]{:S(2)}) %collective-permute-start.5) | collective-permute-done | bytes 147488 | tf_op jit(solution)/shard_map/ppermute | solution.py:142
  16.5 0.8 %shard_map.84.old_ref = f32[24,24,128]{2,1,0:T(8,128)S(1)} custom-call(bf16[576,128]{1,0:T(8,128)(2,1)S(1)} %collective-permute-done.5.x_ref, bf16[128,256]{1,0:T(8,128)(2,1)S(1)} %get-tuple-element.8.both_ref, f32[4,24,24,128]{3,2,1,0:T(8,128)S(1)} %get-tuple-element.9.right_ref, f32[24,24,128]{2,1,0:T(8,128)S(1)} %shard_map.83.old_ref), custom_call_target="tpu_custom_call", output_to_operand_aliasing={{}: (3, {})} | custom-call | tf_op jit(solution)/shard_map/pallas_call | solution.py:112
  17.4 0.0 copy-start
  17.4 0.0 copy-start.1
  17.4 4.9 %collective-permute-done.4.x_ref = bf16[576,128]{1,0:T(8,128)(2,1)S(1)} collective-permute-done((bf16[576,128]{1,0:T(8,128)(2,1)}, bf16[576,128]{1,0:T(8,128)(2,1)S(1)}, u32[]{:S(2)}, u32[]{:S(2)}) %collective-permute-start.4) | collective-permute-done | bytes 147488 | tf_op jit(solution)/shard_map/ppermute | solution.py:142
  22.3 0.8 %shard_map.85.old_ref = f32[24,24,128]{2,1,0:T(8,128)S(1)} custom-call(bf16[576,128]{1,0:T(8,128)(2,1)S(1)} %collective-permute-done.4.x_ref, bf16[128,256]{1,0:T(8,128)(2,1)S(1)} %get-tuple-element.8.both_ref, f32[4,24,24,128]{3,2,1,0:T(8,128)S(1)} %get-tuple-element.9.right_ref, f32[24,24,128]{2,1,0:T(8,128)S(1)} %shard_map.84.old_ref), custom_call_target="tpu_custom_call", output_to_operand_aliasing={{}: (3, {})} | custom-call | tf_op jit(solution)/shard_map/pallas_call | solution.py:112
  23.1 0.0 collective-permute-done.x_ref
  23.1 0.0 copy-done
  23.1 0.0 copy-done.1
  23.1 1.9 %shard_map.86 = bf16[576,128]{1,0:T(8,128)(2,1)} custom-call(bf16[576,128]{1,0:T(8,128)(2,1)S(1)} %collective-permute-done.x_ref, bf16[128,256]{1,0:T(8,128)(2,1)S(1)} %get-tuple-element.8.both_ref, f32[4,24,24,128]{3,2,1,0:T(8,128)S(1)} %get-tuple-element.9.right_ref, f32[24,24,128]{2,1,0:T(8,128)S(1)} %shard_map.85.old_ref, ...), custom_call_target="tpu_custom_call" | custom-call | tf_op jit(solution)/shard_map/pallas_call | solution.py:112
Async XLA Ops:
  0.0 8.0 %collective-permute-start.1 = (bf16[576,128]{1,0:T(8,128)(2,1)}, bf16[576,128]{1,0:T(8,128)(2,1)S(1)}, u32[]{:S(2)}, u32[]{:S(2)}) collective-permute-start(bf16[576,128]{1,0:T(8,128)(2,1)} %bitcast.4), channel_id=1, source_target_pairs={{8,0},{0,8},{24,16},{16,24},{9,1},{1,9},{25,17},{17,25},{10,2},{2,... | collective-permute-start | bytes 442376 | tf_op jit(solution)/shard_map/ppermute | solution.py:134
  1.2 8.7 %collective-permute-start.2 = (bf16[576,128]{1,0:T(8,128)(2,1)}, bf16[576,128]{1,0:T(8,128)(2,1)S(1)}, u32[]{:S(2)}, u32[]{:S(2)}) collective-permute-start(bf16[576,128]{1,0:T(8,128)(2,1)} %bitcast.5), channel_id=1, source_target_pairs={{16,0},{24,8},{0,16},{8,24},{17,1},{25,9},{1,17},{9,25},{18,2},{26... | collective-permute-start | bytes 442376 | tf_op jit(solution)/shard_map/ppermute | solution.py:134
  1.4 8.8 %collective-permute-start.3 = (bf16[576,128]{1,0:T(8,128)(2,1)}, bf16[576,128]{1,0:T(8,128)(2,1)S(1)}, u32[]{:S(2)}, u32[]{:S(2)}) collective-permute-start(bf16[576,128]{1,0:T(8,128)(2,1)} %bitcast.6), channel_id=1, source_target_pairs={{24,0},{16,8},{8,16},{0,24},{25,1},{17,9},{9,17},{1,25},{26,2},{18... | collective-permute-start | bytes 442376 | tf_op jit(solution)/shard_map/ppermute | solution.py:134
  2.6 9.2 %collective-permute-start.6 = (bf16[576,128]{1,0:T(8,128)(2,1)}, bf16[576,128]{1,0:T(8,128)(2,1)S(1)}, u32[]{:S(2)}, u32[]{:S(2)}) collective-permute-start(bf16[576,128]{1,0:T(8,128)(2,1)} %bitcast.7), channel_id=1, source_target_pairs={{16,0},{24,2},{0,4},{8,6},{18,8},{26,10},{2,12},{10,14},{20,16},{2... | collective-permute-start | bytes 442376 | tf_op jit(solution)/shard_map/ppermute | solution.py:142
  2.7 13.8 %collective-permute-start.5 = (bf16[576,128]{1,0:T(8,128)(2,1)}, bf16[576,128]{1,0:T(8,128)(2,1)S(1)}, u32[]{:S(2)}, u32[]{:S(2)}) collective-permute-start(bf16[576,128]{1,0:T(8,128)(2,1)} %bitcast.8), channel_id=1, source_target_pairs={{8,0},{0,2},{24,4},{16,6},{10,8},{2,10},{26,12},{18,14},{12,16},{4... | collective-permute-start | bytes 442376 | tf_op jit(solution)/shard_map/ppermute | solution.py:142
  8.0 14.3 %collective-permute-start.4 = (bf16[576,128]{1,0:T(8,128)(2,1)}, bf16[576,128]{1,0:T(8,128)(2,1)S(1)}, u32[]{:S(2)}, u32[]{:S(2)}) collective-permute-start(bf16[576,128]{1,0:T(8,128)(2,1)} %bitcast.9), channel_id=1, source_target_pairs={{0,0},{8,2},{16,4},{24,6},{2,8},{10,10},{18,12},{26,14},{4,16},{12... | collective-permute-start | bytes 442376 | tf_op jit(solution)/shard_map/ppermute | solution.py:142
  9.9 13.2 %collective-permute-start = (bf16[576,128]{1,0:T(8,128)(2,1)}, bf16[576,128]{1,0:T(8,128)(2,1)S(1)}, u32[]{:S(2)}, u32[]{:S(2)}) collective-permute-start(bf16[576,128]{1,0:T(8,128)(2,1)} %bitcast.10), channel_id=1, source_target_pairs={{24,0},{16,2},{8,4},{0,6},{26,8},{18,10},{10,12},{2,14},{28,16},{2... | collective-permute-start | bytes 442376 | tf_op jit(solution)/shard_map/ppermute | solution.py:142
  17.4 5.7 %copy-start = (bf16[128,128]{1,0:T(8,128)(2,1)S(1)}, bf16[128,128]{1,0:T(8,128)(2,1)}, u32[]{:S(2)}) copy-start(bf16[128,128]{1,0:T(8,128)(2,1)} %out_weight_ref.1) | copy-start | bytes 98308
  17.4 5.7 %copy-start.1 = (f32[128]{0:T(128)S(1)}, f32[128]{0:T(128)}, u32[]{:S(2)}) copy-start(f32[128]{0:T(128)} %param.13) | copy-start | bytes 1540
